TPU v7x, 512 devices: a whole 4x8x8 slice. The times are simulated.
512 devices in a mesh: grp: 8 (over x, y_hi), blk: 64 (over y_lo, z, core).
Axes of the slice: x: 4, y: 8 (y_hi: 2, y_lo: 4; y = y_hi * 4 + y_lo), z: 8, core: 2. Of those that a mesh axis runs over, the one named last changes fastest.
Arguments:
- params: bfloat16 [8, 7168, 4096], P('grp', 'blk'), may hold values from -0.0625 to 0.0625
- tracker: bfloat16 [8, 7168, 4096], P('grp', 'blk'), may hold values from -0.29882812 to 0.29882812
- hidden: bfloat16 [1024, 7168], P('grp', 'blk'), may hold values from -6 to 6
- target: bfloat16 [1024, 4096], P('grp'), may hold values from -6 to 6
Outputs:
- params_next: bfloat16 [8, 7168, 4096], P('grp', 'blk')
- tracker_next: bfloat16 [8, 7168, 4096], P('grp', 'blk')
All inputs are finite; a program needn't handle non-finite values.
Results may differ from a plain program's by a relative error of at most 0.01.
Values may be sent and summed in bfloat16 or wider, within the bound.
A program may use at most 128 MiB of HBM per device.

v0:
```python
import jax
import jax.numpy as jnp
from jax import lax
from jax.sharding import PartitionSpec as P

step_size = 0.05


def from_behind(value, axis, by):
    size = lax.axis_size(axis)
    pairs = [(i, i + by) for i in range(size) if 0 <= i + by < size]
    return lax.ppermute(value, axis, pairs)


def in_blocks(value, dim, size):
    lengths = value.shape
    pieces = value.reshape(*lengths[:dim], size, lengths[dim] // size, *lengths[dim + 1 :])
    return jnp.moveaxis(pieces, dim, 0)


def summed_on_arrival(value, axis, dim):
    pieces = in_blocks(value, dim, lax.axis_size(axis))
    arrived = lax.all_to_all(pieces, axis, split_axis=0, concat_axis=0, tiled=True)
    return arrived.astype(jnp.float32).sum(axis=0)


def sent_to_all(value, axis):
    size = lax.axis_size(axis)
    return lax.all_to_all(
        jnp.broadcast_to(value[None], (size, *value.shape)), axis, 0, 0, tiled=True
    )


def laid_out(pieces, dim):
    lengths = list(pieces.shape[1:])
    lengths[dim] *= pieces.shape[0]
    return jnp.moveaxis(pieces, 0, dim).reshape(lengths)


def collect(value, axis, dim):
    pieces = sent_to_all(value, axis)
    return laid_out(pieces, dim)


def mix_window(window, validity, inner):
    pieces = []
    for place in range(1, inner + 1):
        centre = window[:, place : place + 1]
        left = window[:, place - 1 : place]
        right = window[:, place + 1 : place + 2]
        left_ok = validity[place - 1]
        right_ok = validity[place + 1]
        pieces.append(centre + left_ok * (left - centre) / 3.0 + right_ok * (right - centre) / 3.0)
    return jnp.concatenate(pieces, 1)


def validity_of(width):
    position = lax.axis_index("grp")
    groups = lax.axis_size("grp")
    spots = position - width + jnp.arange(2 * width + 1, dtype=jnp.int32)
    return ((spots >= 0) & (spots < groups)).astype(jnp.float32)


def from_replica(stacked, offset):
    return from_behind(stacked, "grp", offset)


def gradient(weights, hidden, target):
    token_count = hidden.shape[0]
    share = token_count // lax.axis_size("blk")
    section = hidden
    own_output = summed_on_arrival(
        jnp.dot(section, weights, preferred_element_type=jnp.float32).astype(jnp.bfloat16), "blk", 0
    )
    own_target = lax.dynamic_slice_in_dim(target, lax.axis_index("blk") * share, share, 0)
    resid = jnp.tanh(own_output - own_target.astype(jnp.float32)).astype(jnp.bfloat16)
    section = hidden
    total = lax.dot_general(
        section,
        collect(resid, "blk", 0),
        (((0,), (0,)), ((), ())),
        preferred_element_type=jnp.float32,
    )
    return total / token_count


def body(params, tracker, hidden, target):
    grad_old = gradient(params[0], hidden, target)
    stacked = jnp.stack([params, tracker])
    gathered = [
        from_replica(stacked, 2),
        from_replica(stacked, 1),
        stacked,
        from_replica(stacked, -1),
        from_replica(stacked, -2),
    ]
    window = jnp.concatenate(gathered, 1).astype(jnp.float32)
    validity = validity_of(2)
    once = mix_window(window, validity, 3)
    mixed = mix_window(once, validity[1:4], 1)
    params_next = (mixed[0] - step_size * tracker.astype(jnp.float32)).astype(jnp.bfloat16)
    grad_new = gradient(params_next[0], hidden, target)
    tracker_next = (mixed[1] + grad_new[None] - grad_old[None]).astype(jnp.bfloat16)
    return (params_next, tracker_next)


def solution(mesh):
    placed = (P("grp", "blk", None), P("grp", "blk", None), P("grp", "blk"), P("grp", None))
    return jax.shard_map(
        body,
        mesh=mesh,
        in_specs=placed,
        out_specs=(P("grp", "blk", None), P("grp", "blk", None)),
        check_vma=False,
    )
```

profile of v0, /device:TPU:1, one launch (start us, length us, event | category | flops | bytes accessed | tf_op | source)
XLA Modules:
  0.0 339.9 jit_solution(2677421176740184163)
XLA Ops:
  0.7 3.0 pad_maximum_fusion
  3.6 5.2 %collective-permute-start = (bf16[2,1,112,4096]{3,2,1,0:T(8,128)(2,1)}, bf16[2,1,112,4096]{3,2,1,0:T(8,128)(2,1)}, u32[]{:S(2)}, u32[]{:S(2)}) collective-permute-start(bf16[2,1,112,4096]{3,2,1,0:T(8,128)(2,1)} %pad_maximum_fusion), channel_id=1, source_target_pairs={{0,128},{64,192},{128,256},{192,320},{256,384},{320,448},{1,129},{... | collective-permute-start | bytes 5505032 | tf_op jit(solution)/shard_map/ppermute | solution.py:12
  8.8 8.7 %collective-permute-start.1 = (bf16[2,1,112,4096]{3,2,1,0:T(8,128)(2,1)}, bf16[2,1,112,4096]{3,2,1,0:T(8,128)(2,1)}, u32[]{:S(2)}, u32[]{:S(2)}) collective-permute-start(bf16[2,1,112,4096]{3,2,1,0:T(8,128)(2,1)} %pad_maximum_fusion), channel_id=1, source_target_pairs={{0,64},{64,128},{128,192},{192,256},{256,320},{320,384},{384,448},... | collective-permute-start | bytes 5505032 | tf_op jit(solution)/shard_map/ppermute | solution.py:12
  20.6 1.5 reshape.24
  22.1 12.4 %all-to-all-start.2 = ((bf16[64,2,4096]{2,1,0:T(2,128)(2,1)}), bf16[64,2,4096]{2,1,0:T(2,128)(2,1)S(1)}, u32[]{:S(2)}, u32[]{:S(2)}) async-start(bf16[64,2,4096]{2,1,0:T(2,128)(2,1)} %reshape.24), calls=%async_computation.2 | async-start | bytes 2097152 | tf_op jit(solution)/shard_map/all_to_all | solution.py:23
  35.2 46.7 %collective-permute-done = bf16[2,1,112,4096]{3,2,1,0:T(8,128)(2,1)} collective-permute-done((bf16[2,1,112,4096]{3,2,1,0:T(8,128)(2,1)}, bf16[2,1,112,4096]{3,2,1,0:T(8,128)(2,1)}, u32[]{:S(2)}, u32[]{:S(2)}) %collective-permute-start) | collective-permute-done | bytes 1835040 | tf_op jit(solution)/shard_map/ppermute | solution.py:12
  81.9 2.9 constant_dynamic-update-slice_fusion.4
  84.9 2.9 constant_dynamic-update-slice_fusion.3
  87.8 1.4 constant_dynamic-update-slice_fusion.2
  89.2 46.1 %collective-permute-done.2 = bf16[2,1,112,4096]{3,2,1,0:T(8,128)(2,1)} collective-permute-done((bf16[2,1,112,4096]{3,2,1,0:T(8,128)(2,1)}, bf16[2,1,112,4096]{3,2,1,0:T(8,128)(2,1)}, u32[]{:S(2)}, u32[]{:S(2)}) %collective-permute-start.2) | collective-permute-done | bytes 1835040 | tf_op jit(solution)/shard_map/ppermute | solution.py:12
  135.3 3.0 constant_dynamic-update-slice_fusion.1
  138.3 3.0 constant_dynamic-update-slice_fusion
  141.3 12.4 %convert_element_type.43 = f32[2,5,112,4096]{3,2,1,0:T(8,128)} convert(bf16[2,5,112,4096]{3,2,1,0:T(8,128)(2,1)} %constant_dynamic-update-slice_fusion) | non-fusion elementwise | flops 4587520 | bytes 27525120 | tf_op jit(solution)/shard_map/convert_element_type | solution.py:97
  153.6 11.3 %fusion.13 = f32[2,1,112,4096]{3,2,1,0:T(8,128)S(1)} fusion(f32[2,5,112,4096]{3,2,1,0:T(8,128)} %convert_element_type.43, f32[]{:T(128)} %bitcast.6, f32[]{:T(128)} %bitcast.5, f32[]{:T(128)} %bitcast.4, f32[]{:T(128)} %bitcast.3, f32[]{:T(128)} %bitcast.2), kind=kLoop, calls=%fused_computation.18 | loop fusion | flops 29360128 | bytes 22020116 | tf_op jit(solution)/shard_map/add | solution.py:53
  165.0 1.8 copy-done.1
  168.4 1.5 reshape.22
  169.9 64.7 %all-to-all-start = ((bf16[64,2,4096]{2,1,0:T(2,128)(2,1)}), bf16[64,2,4096]{2,1,0:T(2,128)(2,1)S(1)}, u32[]{:S(2)}, u32[]{:S(2)}) async-start(bf16[64,2,4096]{2,1,0:T(2,128)(2,1)} %reshape.22), calls=%async_computation | async-start | bytes 2097152 | tf_op jit(solution)/shard_map/all_to_all | solution.py:23
  235.5 27.8 %all-to-all-done = bf16[64,2,4096]{2,1,0:T(2,128)(2,1)S(1)} async-done(((bf16[64,2,4096]{2,1,0:T(2,128)(2,1)}), bf16[64,2,4096]{2,1,0:T(2,128)(2,1)S(1)}, u32[]{:S(2)}, u32[]{:S(2)}) %all-to-all-start) | async-done | bytes 1048608 | tf_op jit(solution)/shard_map/all_to_all | solution.py:23
  266.1 34.4 %all_to_all.20 = bf16[64,2,4096]{2,1,0:T(2,128)(2,1)S(1)} all-to-all(bf16[64,2,4096]{2,1,0:T(2,128)(2,1)S(1)} %broadcast_in_dim.4), channel_id=1, replica_groups=mesh['grp'=8,'blk'=64] {'blk'}, dimensions={0} | all-to-all | bytes 2097152 | tf_op jit(solution)/shard_map/all_to_all | solution.py:29
  300.4 2.0 broadcast_in_dim.5
  302.5 6.0 %all-to-all-start.3 = ((bf16[64,2,4096]{2,1,0:T(2,128)(2,1)}), bf16[64,2,4096]{2,1,0:T(2,128)(2,1)}, u32[]{:S(2)}, u32[]{:S(2)}) async-start(bf16[64,2,4096]{2,1,0:T(2,128)(2,1)} %broadcast_in_dim.5), calls=%async_computation.3 | async-start | bytes 2097152 | tf_op jit(solution)/shard_map/all_to_all | solution.py:29
  308.9 1.9 fusion.3
  310.9 26.2 %all-to-all-done.3 = bf16[64,2,4096]{2,1,0:T(2,128)(2,1)} async-done(((bf16[64,2,4096]{2,1,0:T(2,128)(2,1)}), bf16[64,2,4096]{2,1,0:T(2,128)(2,1)}, u32[]{:S(2)}, u32[]{:S(2)}) %all-to-all-start.3) | async-done | bytes 1048608 | tf_op jit(solution)/shard_map/all_to_all | solution.py:29
  337.1 1.5 reshape.25
  (25 shorter events, 10.7 us)
Async XLA Ops:
  0.6 19.5 %copy-start = (bf16[128,112]{0,1:T(8,128)(2,1)S(1)}, bf16[128,112]{0,1:T(8,128)(2,1)}, u32[]{:S(2)}) copy-start(bf16[128,112]{0,1:T(8,128)(2,1)} %param.6) | copy-start | bytes 86020
  0.6 19.5 %copy-start.3 = (bf16[1,112,4096]{2,1,0:T(8,128)(2,1)S(1)}, bf16[1,112,4096]{2,1,0:T(8,128)(2,1)}, u32[]{:S(2)}) copy-start(bf16[1,112,4096]{2,1,0:T(8,128)(2,1)} %param.4) | copy-start | bytes 2752516
  3.6 78.3 %collective-permute-start = (bf16[2,1,112,4096]{3,2,1,0:T(8,128)(2,1)}, bf16[2,1,112,4096]{3,2,1,0:T(8,128)(2,1)}, u32[]{:S(2)}, u32[]{:S(2)}) collective-permute-start(bf16[2,1,112,4096]{3,2,1,0:T(8,128)(2,1)} %pad_maximum_fusion), channel_id=1, source_target_pairs={{0,128},{64,192},{128,256},{192,320},{256,384},{320,448},{1,129},{... | collective-permute-start | bytes 5505032 | tf_op jit(solution)/shard_map/ppermute | solution.py:12
  8.8 76.0 %collective-permute-start.1 = (bf16[2,1,112,4096]{3,2,1,0:T(8,128)(2,1)}, bf16[2,1,112,4096]{3,2,1,0:T(8,128)(2,1)}, u32[]{:S(2)}, u32[]{:S(2)}) collective-permute-start(bf16[2,1,112,4096]{3,2,1,0:T(8,128)(2,1)} %pad_maximum_fusion), channel_id=1, source_target_pairs={{0,64},{64,128},{128,192},{192,256},{256,320},{320,384},{384,448},... | collective-permute-start | bytes 5505032 | tf_op jit(solution)/shard_map/ppermute | solution.py:12
  17.5 117.8 %collective-permute-start.2 = (bf16[2,1,112,4096]{3,2,1,0:T(8,128)(2,1)}, bf16[2,1,112,4096]{3,2,1,0:T(8,128)(2,1)}, u32[]{:S(2)}, u32[]{:S(2)}) collective-permute-start(bf16[2,1,112,4096]{3,2,1,0:T(8,128)(2,1)} %pad_maximum_fusion), channel_id=1, source_target_pairs={{64,0},{128,64},{192,128},{256,192},{320,256},{384,320},{448,384},... | collective-permute-start | bytes 5505032 | tf_op jit(solution)/shard_map/ppermute | solution.py:12
  18.8 119.5 %collective-permute-start.3 = (bf16[2,1,112,4096]{3,2,1,0:T(8,128)(2,1)}, bf16[2,1,112,4096]{3,2,1,0:T(8,128)(2,1)}, u32[]{:S(2)}, u32[]{:S(2)}) collective-permute-start(bf16[2,1,112,4096]{3,2,1,0:T(8,128)(2,1)} %pad_maximum_fusion), channel_id=1, source_target_pairs={{128,0},{192,64},{256,128},{320,192},{384,256},{448,320},{129,1},{... | collective-permute-start | bytes 5505032 | tf_op jit(solution)/shard_map/ppermute | solution.py:12
  22.1 147.8 %all-to-all-start.2 = ((bf16[64,2,4096]{2,1,0:T(2,128)(2,1)}), bf16[64,2,4096]{2,1,0:T(2,128)(2,1)S(1)}, u32[]{:S(2)}, u32[]{:S(2)}) async-start(bf16[64,2,4096]{2,1,0:T(2,128)(2,1)} %reshape.24), calls=%async_computation.2 | async-start | bytes 2097152 | tf_op jit(solution)/shard_map/all_to_all | solution.py:23
  35.2 52.5 %copy-start.2 = (bf16[1,112,4096]{2,1,0:T(8,128)(2,1)S(1)}, bf16[1,112,4096]{2,1,0:T(8,128)(2,1)}, u32[]{:S(2)}) copy-start(bf16[1,112,4096]{2,1,0:T(8,128)(2,1)} %param.5) | copy-start | bytes 2752516
  165.0 1.8 copy-start.1
  167.0 0.9 copy-start.4
  169.9 93.4 %all-to-all-start = ((bf16[64,2,4096]{2,1,0:T(2,128)(2,1)}), bf16[64,2,4096]{2,1,0:T(2,128)(2,1)S(1)}, u32[]{:S(2)}, u32[]{:S(2)}) async-start(bf16[64,2,4096]{2,1,0:T(2,128)(2,1)} %reshape.22), calls=%async_computation | async-start | bytes 2097152 | tf_op jit(solution)/shard_map/all_to_all | solution.py:23
  302.5 34.7 %all-to-all-start.3 = ((bf16[64,2,4096]{2,1,0:T(2,128)(2,1)}), bf16[64,2,4096]{2,1,0:T(2,128)(2,1)}, u32[]{:S(2)}, u32[]{:S(2)}) async-start(bf16[64,2,4096]{2,1,0:T(2,128)(2,1)} %broadcast_in_dim.5), calls=%async_computation.3 | async-start | bytes 2097152 | tf_op jit(solution)/shard_map/all_to_all | solution.py:29
where the time goes:
time: 341 us; the launch traced here: 340 us
  waiting for transfers between devices  147 us (43%)
  starting transfers between devices  99.7 us (29%)
  blocking collectives  34.4 us (10%)
  other arithmetic  30.9 us (9%)
  local copies, waits for them, and re-layouts  23.1 us (7%)
  matrix products  4.18 us (1%)
    ppermute x4, waiting for transfers between devices, from_behind(): return lax.ppermute(value, axis, pairs)  92.8 us
    all_to_all x2, starting transfers between devices, summed_on_arrival(): lax.all_to_all(pieces, axis, split_axis=0, concat_axis=0, tiled=True)  77.2 us
    all_to_all x1, blocking collectives, sent_to_all(): lax.all_to_all(jnp.broadcast_to(value[None], (size, *value.shape)), axis,...  34.4 us
    all_to_all x2, waiting for transfers between devices, summed_on_arrival(): lax.all_to_all(pieces, axis, split_axis=0, concat_axis=0, tiled=True)  27.8 us
    all_to_all x1, waiting for transfers between devices, sent_to_all(): lax.all_to_all(jnp.broadcast_to(value[None], (size, *value.shape)), axis,...  26.2 us
    ppermute x4, starting transfers between devices, from_behind(): return lax.ppermute(value, axis, pairs)  16.5 us
    convert_element_type x1, other arithmetic, body(): window = jnp.concatenate(gathered, 1).astype(jnp.float32)  12.4 us
    unnamed x13, local copies, waits for them, and re-layouts  11.5 us
  transfers between devices with their start and end apart: 7, of which 4 were waited for; matrix products, arithmetic and copies ran while one was open for 13% of the time, Pallas kernels for 0%

commit v1 on v0

v1 whole, which is shorter than its diff:
```python
import jax
import jax.numpy as jnp
from jax import lax
from jax.experimental import pallas as pl
from jax.experimental.pallas import tpu as pltpu
from jax.sharding import PartitionSpec as P

step_size = 0.05
MESH = pl.DeviceIdType.MESH
F32 = jnp.float32
BF16 = jnp.bfloat16

RUN = 4
RING = 8
CORES = 2
CHUNK = 1024
HALF = CHUNK // CORES
PIECE = HALF // RUN


def step_kernel(
    params, tracker, hidden, target,
    params_next, tracker_next,
    p_own, t_own, h_own, tgt, h_turned,
    p_across, p_side, u_out, u_in, p_new,
    t_side, w_out, w_in, t_new,
    grad,
    core_out, core_keep, core_in, z_out, z_in, y_out, y_in, resid_old,
    gather_own, gather_other,
    in_sem, out_sem,
    pair_s, pair_r, row_s, row_r, u_s, u_r, tx_s, tx_r, ty_s, ty_r,
    core_s, core_r, z_s, z_r, y_s, y_r, gy_s, gy_r, gz_s, gz_r, gc_s, gc_r,
):
    rows, width = p_own.shape
    tokens = h_own.shape[0]
    strip = tokens // RING
    steps = width // CHUNK
    blocks = width // HALF
    group, place = lax.axis_index("grp"), lax.axis_index("blk")
    n_grp = lax.axis_size("grp")
    columns = n_grp // 2
    x, side = group // 2, lax.rem(group, 2)
    run, rest = place // (RING * CORES), lax.rem(place, RING * CORES)
    ring, core = rest // CORES, lax.rem(rest, CORES)
    s = 1 - 2 * side

    def at_blk(run_, ring_, core_):
        return (group, (run_ * RING + ring_) * CORES + core_)

    partner = at_blk(run, ring, 1 - core)
    ring_peer = [at_blk(run, lax.rem(ring + j, RING), core) for j in range(1, RING)]
    ring_at = [lax.rem(ring + j, RING) for j in range(1, RING)]
    run_peer = [at_blk(lax.rem(run + j, RUN), ring, core) for j in range(1, RUN)]
    run_at = [lax.rem(run + j, RUN) for j in range(1, RUN)]
    across = (x * 2 + (1 - side), place)
    ahead = (lax.rem(x + s + columns, columns) * 2 + side, place)
    behind = (lax.rem(x - s + columns, columns) * 2 + side, place)

    barrier = pltpu.get_barrier_semaphore()
    peers = [across, ahead, behind, partner] + run_peer + ring_peer
    for peer in peers:
        pl.semaphore_signal(barrier, inc=1, device_id=peer, device_id_type=MESH)

    def piece_column(k):
        return pl.multiple_of(k * CHUNK + core * HALF + run * PIECE, PIECE)

    ring_rows = pl.ds(pl.multiple_of(ring * strip, strip), strip)
    loads = [
        pltpu.make_async_copy(params, p_own, in_sem.at[0]),
        pltpu.make_async_copy(tracker, t_own, in_sem.at[1]),
        pltpu.make_async_copy(hidden, h_own, in_sem.at[2]),
    ] + [
        pltpu.make_async_copy(
            target.at[ring_rows, pl.ds(piece_column(k), PIECE)], tgt.at[k], in_sem.at[3 + k]
        )
        for k in range(steps)
    ]
    for load in loads:
        load.start()

    def remote(src, dst, send, recv, peer):
        return pltpu.make_async_remote_copy(
            src_ref=src, dst_ref=dst, send_sem=send, recv_sem=recv, device_id=peer, device_id_type=MESH
        )

    def cols(k, w):
        return pl.ds(k * w, w)

    def valid(i):
        return jnp.where((i >= 0) & (i < n_grp), 1.0, 0.0).astype(F32)

    def keep(i):
        return 1.0 - (valid(i - 1) + valid(i + 1)) / 3.0

    third = 1.0 / 3.0
    c_own = keep(group) * keep(group) + (valid(group - 1) + valid(group + 1)) / 9.0
    c_pair = (keep(group) + keep(group + s)) * third
    c_ahead = valid(group + 2 * s) / 9.0
    c_behind = valid(group - 2 * s) / 9.0
    c_next = (keep(group + s) + keep(group + 2 * s)) * third * valid(group + 2 * s)

    sent = []

    def go(copy):
        copy.start()
        sent.append(copy)
        return copy

    pair, row, u, tx, ty = {}, {}, {}, {}, {}
    core_copy, z_copy, y_copy, gy, gz, gc = {}, {}, {}, {}, {}, {}
    outs = []

    def send_tx(k, d):
        c = cols(k, CHUNK)
        tx[k, d] = go(remote(
            t_own.at[:, c], t_side.at[d, :, c], tx_s.at[d, k], tx_r.at[d, k], behind if d == 0 else ahead
        ))

    def outputs(p, k):
        weights = p_own if p == 0 else p_new
        for half in range(CORES):
            c = cols(k * CORES + half, HALF)
            part = jnp.dot(h_own[...], weights[:, c], preferred_element_type=F32)
            core_keep[p, k, half] = part
            core_out[p, k, half] = part.astype(BF16)
        core_copy[p, k] = go(remote(
            core_out.at[p, k, 1 - core], core_in.at[p, k], core_s.at[p, k], core_r.at[p, k], partner
        ))

    def across_ring(p, k):
        core_copy[p, k].wait_recv()
        z_out[p, k] = (core_keep[p, k, core] + core_in[p, k].astype(F32)).astype(BF16)
        for j in range(RING - 1):
            part = pl.ds(pl.multiple_of(ring_at[j] * strip, strip), strip)
            z_copy[p, k, j] = go(remote(
                z_out.at[p, k, part], z_in.at[p, k, j], z_s.at[p, k, j], z_r.at[p, k, j], ring_peer[j]
            ))

    def across_run(p, k):
        total = z_out[p, k, ring_rows].astype(F32)
        for j in range(RING - 1):
            z_copy[p, k, j].wait_recv()
            total += z_in[p, k, j].astype(F32)
        y_out[p, k] = total.astype(BF16)
        for j in range(RUN - 1):
            part = pl.ds(pl.multiple_of(run_at[j] * PIECE, PIECE), PIECE)
            y_copy[p, k, j] = go(remote(
                y_out.at[p, k, :, part], y_in.at[p, k, j], y_s.at[p, k, j], y_r.at[p, k, j], run_peer[j]
            ))

    own_piece = pl.ds(pl.multiple_of(run * PIECE, PIECE), PIECE)

    def residual(p, k):
        total = y_out[p, k, :, own_piece].astype(F32)
        for j in range(RUN - 1):
            y_copy[p, k, j].wait_recv()
            total += y_in[p, k, j].astype(F32)
        resid = jnp.tanh(total - tgt[k].astype(F32))
        if p == 0:
            resid_old[k] = resid
            return
        gather_own[k, ring_rows, own_piece] = (resid - resid_old[k]).astype(BF16)
        block = gather_own.at[k, ring_rows, own_piece]
        for j in range(RUN - 1):
            gy[k, j] = go(remote(block, block, gy_s.at[k, j], gy_r.at[k, j], run_peer[j]))

    def back_ring(k):
        for j in range(RUN - 1):
            gy[k, j].wait_recv()
        block = gather_own.at[k, ring_rows]
        for j in range(RING - 1):
            gz[k, j] = go(remote(block, block, gz_s.at[k, j], gz_r.at[k, j], ring_peer[j]))

    def back_core(k):
        for j in range(RING - 1):
            gz[k, j].wait_recv()
        gc[k] = go(remote(gather_own.at[k], gather_other.at[k], gc_s.at[k], gc_r.at[k], partner))
        c = pl.ds(pl.multiple_of(k * CHUNK + core * HALF, HALF), HALF)
        grad[:, c] = jnp.dot(h_turned[...], gather_own[k], preferred_element_type=F32)

    def last_grad(k):
        gc[k].wait_recv()
        c = pl.ds(pl.multiple_of(k * CHUNK + (1 - core) * HALF, HALF), HALF)
        grad[:, c] = jnp.dot(h_turned[...], gather_other[k], preferred_element_type=F32)

    def send_u(k):
        c = cols(k, CHUNK)
        pair[k].wait_recv()
        u_out[:, c] = (c_ahead * p_own[:, c].astype(F32) + c_next * p_across[:, c].astype(F32)).astype(BF16)
        u[k] = go(remote(u_out.at[:, c], u_in.at[:, c], u_s.at[k], u_r.at[k], ahead))

    def new_params(k):
        c = cols(k, CHUNK)
        row[k].wait_recv()
        u[k].wait_recv()
        mixed = c_own * p_own[:, c].astype(F32) + c_pair * p_across[:, c].astype(F32)
        mixed += c_ahead * p_side[:, c].astype(F32) + u_in[:, c].astype(F32)
        p_new[:, c] = (mixed - step_size * t_own[:, c].astype(F32)).astype(BF16)
        store = pltpu.make_async_copy(p_new.at[:, c], params_next.at[:, c], out_sem.at[0, k])
        store.start()
        outs.append(store)

    seen = set()

    def send_ty(b):
        k = b * HALF // CHUNK
        if k not in seen:
            tx[k, 0].wait_recv()
            seen.add(k)
        c = cols(b, HALF)
        w_out[:, c] = (c_pair * t_own[:, c].astype(F32) + c_next * t_side[0, :, c].astype(F32)).astype(BF16)
        ty[b] = go(remote(w_out.at[:, c], w_in.at[:, c], ty_s.at[b], ty_r.at[b], across))

    def new_tracker(b):
        c = cols(b, HALF)
        ty[b].wait_recv()
        mixed = c_own * t_own[:, c].astype(F32) + c_ahead * t_side[0, :, c].astype(F32)
        mixed += c_behind * t_side[1, :, c].astype(F32) + w_in[:, c].astype(F32)
        t_new[:, c] = (mixed + grad[:, c] * (1.0 / tokens)).astype(BF16)
        store = pltpu.make_async_copy(t_new.at[:, c], tracker_next.at[:, c], out_sem.at[1, b])
        store.start()
        outs.append(store)

    loads[0].wait()
    pl.semaphore_wait(barrier, len(peers))
    for k in range(steps):
        c = cols(k, CHUNK)
        pair[k] = go(remote(p_own.at[:, c], p_across.at[:, c], pair_s.at[k], pair_r.at[k], across))
    for k in range(steps):
        c = cols(k, CHUNK)
        row[k] = go(remote(p_own.at[:, c], p_side.at[:, c], row_s.at[k], row_r.at[k], behind))
    loads[1].wait()
    for k in range(steps):
        send_tx(k, 0)
    for k in range(2):
        send_tx(k, 1)
    loads[2].wait()
    h_turned[...] = h_own[...].astype(F32).T.astype(BF16)
    for load in loads[3:]:
        load.wait()
    for k in range(steps):
        outputs(0, k)
    for k in range(steps):
        across_ring(0, k)
    send_u(0)
    send_tx(2, 1)
    for k in range(steps):
        across_run(0, k)
    new_params(0)
    outputs(1, 0)
    across_ring(1, 0)
    send_u(1)
    send_tx(3, 1)
    new_params(1)
    outputs(1, 1)
    across_ring(1, 1)
    across_run(1, 0)
    send_u(2)
    new_params(2)
    outputs(1, 2)
    across_ring(1, 2)
    across_run(1, 1)
    send_ty(0)
    send_ty(1)
    send_u(3)
    new_params(3)
    outputs(1, 3)
    across_ring(1, 3)
    for k in range(steps):
        residual(0, k)
    residual(1, 0)
    residual(1, 1)
    across_run(1, 2)
    send_ty(2)
    back_ring(0)
    back_ring(1)
    across_run(1, 3)
    send_ty(3)
    residual(1, 2)
    residual(1, 3)
    send_ty(4)
    send_ty(5)
    send_ty(6)
    send_ty(7)
    back_ring(2)
    back_core(0)
    back_core(1)
    last_grad(0)
    last_grad(1)
    back_ring(3)
    back_core(2)
    last_grad(2)
    for k in range(steps):
        tx[k, 1].wait_recv()
    for b in range(4):
        new_tracker(b)
    back_core(3)
    last_grad(3)
    for b in range(4, blocks):
        new_tracker(b)
    for copy in sent:
        copy.wait_send()
    for store in outs:
        store.wait()


def body(params, tracker, hidden, target):
    _, rows, width = params.shape
    tokens = hidden.shape[0]
    steps, blocks = width // CHUNK, width // HALF
    strip = tokens // RING
    any_ = pl.BlockSpec(memory_space=pl.ANY)
    dma = pltpu.SemaphoreType.DMA
    whole = pltpu.VMEM((rows, width), BF16)
    scratch = [
        whole, whole, pltpu.VMEM(hidden.shape, BF16), pltpu.VMEM((steps, strip, PIECE), BF16),
        pltpu.VMEM((rows, tokens), BF16),
        whole, whole, whole, whole, whole,
        pltpu.VMEM((2, rows, width), BF16), whole, whole, whole,
        pltpu.VMEM((rows, width), F32),
        pltpu.VMEM((2, steps, CORES, tokens, HALF), BF16), pltpu.VMEM((2, steps, CORES, tokens, HALF), F32),
        pltpu.VMEM((2, steps, tokens, HALF), BF16), pltpu.VMEM((2, steps, tokens, HALF), BF16),
        pltpu.VMEM((2, steps, RING - 1, strip, HALF), BF16),
        pltpu.VMEM((2, steps, strip, HALF), BF16), pltpu.VMEM((2, steps, RUN - 1, strip, PIECE), BF16),
        pltpu.VMEM((steps, strip, PIECE), F32),
        pltpu.VMEM((steps, tokens, HALF), BF16), pltpu.VMEM((steps, tokens, HALF), BF16),
        dma((3 + steps,)), dma((2, blocks)),
    ]
    for shape in (
        (steps,), (steps,), (steps,), (2, steps), (blocks,),
        (2, steps), (2, steps, RING - 1), (2, steps, RUN - 1),
        (steps, RUN - 1), (steps, RING - 1), (steps,),
    ):
        scratch += [dma(shape), dma(shape)]
    out = jax.ShapeDtypeStruct((rows, width), BF16)
    params_next, tracker_next = pl.pallas_call(
        step_kernel,
        out_shape=(out, out),
        in_specs=[any_] * 4,
        out_specs=(any_, any_),
        scratch_shapes=scratch,
        name="tracking_step",
        compiler_params=pltpu.CompilerParams(collective_id=0, has_side_effects=True, vmem_limit_bytes=60 << 20),
    )(params[0], tracker[0], hidden, target)
    return params_next[None], tracker_next[None]


def solution(mesh):
    placed = (P("grp", "blk", None), P("grp", "blk", None), P("grp", "blk"), P("grp", None))
    return jax.shard_map(
        body,
        mesh=mesh,
        in_specs=placed,
        out_specs=(P("grp", "blk", None), P("grp", "blk", None)),
        check_vma=False,
    )
```

time: 341 us -> 125 us (0.37)
  waiting for transfers between devices: 147 us -> 0 us
  Pallas kernels: 0 us -> 119 us
  starting transfers between devices: 99.7 us -> 0 us
  blocking collectives: 34.4 us -> 0 us
  other arithmetic: 30.9 us -> 0 us
  local copies, waits for them, and re-layouts: 23.1 us -> 4.64 us
  matrix products: 4.18 us -> 0 us
    pallas_call x0 -> x1, Pallas kernels: none -> 119 us  [body(): pl.pallas_call(step_kernel, out_shape=(out, out), in_specs=[any_] * 4, ou...]
    ppermute x4 -> x0, waiting for transfers between devices: 92.8 us -> none  [from_behind(): return lax.ppermute(value, axis, pairs)]
    all_to_all x3 -> x0, starting transfers between devices: 83.2 us -> none  [the longest x2 77.2 us: summed_on_arrival(): lax.all_to_all(pieces, axis, split_axis=0, concat_axis=0, tiled=True)]
    all_to_all x3 -> x0, waiting for transfers between devices: 54 us -> none  [the longest x2 27.8 us: summed_on_arrival(): lax.all_to_all(pieces, axis, split_axis=0, concat_axis=0, tiled=True)]
    all_to_all x1 -> x0, blocking collectives: 34.4 us -> none  [sent_to_all(): lax.all_to_all(jnp.broadcast_to(value[None], (size, *value.shape)), axis,...]
    ppermute x4 -> x0, starting transfers between devices: 16.5 us -> none  [from_behind(): return lax.ppermute(value, axis, pairs)]
    convert_element_type x4 -> x0, other arithmetic: 13.5 us -> none  [the longest x1 12.4 us: body(): window = jnp.concatenate(gathered, 1).astype(jnp.float32)]
    add x1 -> x0, other arithmetic: 11.3 us -> none  [mix_window(): centre + left_ok * (left - centre) / 3.0 + right_ok * (right - centre) / 3.0]
  transfers between devices with their start and end apart: 7 -> 0, of which waited for: 4 -> 0; matrix products, arithmetic and copies ran while one was open for 13% -> 0% of each run, Pallas kernels for 0% -> 0%
where the time goes in v1:
time: 125 us
  Pallas kernels  119 us (95%)
  local copies, waits for them, and re-layouts  4.64 us (4%)
    pallas_call x1, Pallas kernels, body(): pl.pallas_call(step_kernel, out_shape=(out, out), in_specs=[any_] * 4, ou...  119 us
    unnamed x5, local copies, waits for them, and re-layouts  4.64 us

profile of v1, /device:TPU:1, one launch (start us, length us, event | category | flops | bytes accessed | tf_op | source)
XLA Modules:
  0.0 124.7 jit_solution(12828821333163730093)
XLA Ops:
  0.6 1.5 %copy.6.hidden = bf16[128,112]{1,0:T(8,128)(2,1)} copy(bf16[128,112]{0,1:T(8,128)(2,1)} %param.6) | data formatting | bytes 57344 | tf_op args[2]
  2.1 119.4 %tracking_step.1 = (bf16[112,4096]{1,0:T(8,128)(2,1)}, bf16[112,4096]{1,0:T(8,128)(2,1)}) custom-call(bf16[112,4096]{1,0:T(8,128)(2,1)} %bitcast.6, bf16[112,4096]{1,0:T(8,128)(2,1)} %bitcast.7, bf16[128,112]{1,0:T(8,128)(2,1)} %copy.6.hidden, bf16[128,4096]{1,0:T(8,128)(2,1)} %target.1), custom_call_target="tpu_custom_call" | custom-call | tf_op jit(solution)/shard_map/tracking_step/pallas_call | solution.py:336
  121.5 0.0 copy-start
  121.5 2.2 %copy.9 = bf16[1,112,4096]{2,1,0:T(8,128)(2,1)} copy(bf16[1,112,4096]{2,1,0:T(8,128)(2,1)} %bitcast.5) | data formatting | bytes 1835008
  123.7 0.0 copy-done
  123.7 0.9 copy.10
Async XLA Ops:
  121.5 2.3 %copy-start = (bf16[112,4096]{1,0:T(8,128)(2,1)S(1)}, bf16[112,4096]{1,0:T(8,128)(2,1)}, u32[]{:S(2)}) copy-start(bf16[112,4096]{1,0:T(8,128)(2,1)} %get-tuple-element.5) | copy-start | bytes 2752516

commit v2 on v1

--- a/solution.py
+++ b/solution.py
@@ -13,6 +13,8 @@
 RUN = 4
 RING = 8
 CORES = 2
+SCOPES = False
+RAW = 2
 CHUNK = 1024
 HALF = CHUNK // CORES
 PIECE = HALF // RUN
@@ -22,12 +24,12 @@
     params, tracker, hidden, target,
     params_next, tracker_next,
     p_own, t_own, h_own, tgt, h_turned,
-    p_across, p_side, u_out, u_in, p_new,
-    t_side, w_out, w_in, t_new,
+    p_across, p_side, u_out, u_in,
+    t_side, w_out, w_in,
     grad,
     core_out, core_keep, core_in, z_out, z_in, y_out, y_in, resid_old,
     gather_own, gather_other,
-    in_sem, out_sem,
+    in_sem,
     pair_s, pair_r, row_s, row_r, u_s, u_r, tx_s, tx_r, ty_s, ty_r,
     core_s, core_r, z_s, z_r, y_s, y_r, gy_s, gy_r, gz_s, gz_r, gc_s, gc_r,
 ):
@@ -68,7 +70,7 @@
     loads = [
         pltpu.make_async_copy(params, p_own, in_sem.at[0]),
         pltpu.make_async_copy(tracker, t_own, in_sem.at[1]),
-        pltpu.make_async_copy(hidden, h_own, in_sem.at[2]),
+        pltpu.make_async_copy(hidden, h_turned, in_sem.at[2]),
     ] + [
         pltpu.make_async_copy(
             target.at[ring_rows, pl.ds(piece_column(k), PIECE)], tgt.at[k], in_sem.at[3 + k]
@@ -108,7 +110,6 @@
 
     pair, row, u, tx, ty = {}, {}, {}, {}, {}
     core_copy, z_copy, y_copy, gy, gz, gc = {}, {}, {}, {}, {}, {}
-    outs = []
 
     def send_tx(k, d):
         c = cols(k, CHUNK)
@@ -117,7 +118,7 @@
         ))
 
     def outputs(p, k):
-        weights = p_own if p == 0 else p_new
+        weights = p_own if p == 0 else params_next
         for half in range(CORES):
             c = cols(k * CORES + half, HALF)
             part = jnp.dot(h_own[...], weights[:, c], preferred_element_type=F32)
@@ -189,16 +190,26 @@
         u_out[:, c] = (c_ahead * p_own[:, c].astype(F32) + c_next * p_across[:, c].astype(F32)).astype(BF16)
         u[k] = go(remote(u_out.at[:, c], u_in.at[:, c], u_s.at[k], u_r.at[k], ahead))
 
+    def send_pair(k):
+        c = cols(k, CHUNK)
+        block = p_own
+        if k >= RAW:
+            row[k].wait_recv()
+            block = u_out
+            u_out[:, c] = (c_pair * p_own[:, c].astype(F32) + c_next * p_side[:, c].astype(F32)).astype(BF16)
+        pair[k] = go(remote(block.at[:, c], p_across.at[:, c], pair_s.at[k], pair_r.at[k], across))
+
     def new_params(k):
         c = cols(k, CHUNK)
-        row[k].wait_recv()
+        mixed = c_own * p_own[:, c].astype(F32) - step_size * t_own[:, c].astype(F32)
         u[k].wait_recv()
-        mixed = c_own * p_own[:, c].astype(F32) + c_pair * p_across[:, c].astype(F32)
-        mixed += c_ahead * p_side[:, c].astype(F32) + u_in[:, c].astype(F32)
-        p_new[:, c] = (mixed - step_size * t_own[:, c].astype(F32)).astype(BF16)
-        store = pltpu.make_async_copy(p_new.at[:, c], params_next.at[:, c], out_sem.at[0, k])
-        store.start()
-        outs.append(store)
+        if k < RAW:
+            row[k].wait_recv()
+            mixed += c_pair * p_across[:, c].astype(F32) + u_in[:, c].astype(F32)
+        else:
+            pair[k].wait_recv()
+            mixed += p_across[:, c].astype(F32) + c_behind * u_in[:, c].astype(F32)
+        params_next[:, c] = (mixed + c_ahead * p_side[:, c].astype(F32)).astype(BF16)
 
     seen = set()
 
@@ -216,92 +227,91 @@
         ty[b].wait_recv()
         mixed = c_own * t_own[:, c].astype(F32) + c_ahead * t_side[0, :, c].astype(F32)
         mixed += c_behind * t_side[1, :, c].astype(F32) + w_in[:, c].astype(F32)
-        t_new[:, c] = (mixed + grad[:, c] * (1.0 / tokens)).astype(BF16)
-        store = pltpu.make_async_copy(t_new.at[:, c], tracker_next.at[:, c], out_sem.at[1, b])
-        store.start()
-        outs.append(store)
+        tracker_next[:, c] = (mixed + grad[:, c] * (1.0 / tokens)).astype(BF16)
 
     loads[0].wait()
     pl.semaphore_wait(barrier, len(peers))
+    for k in range(RAW):
+        send_pair(k)
     for k in range(steps):
         c = cols(k, CHUNK)
-        pair[k] = go(remote(p_own.at[:, c], p_across.at[:, c], pair_s.at[k], pair_r.at[k], across))
-    for k in range(steps):
-        c = cols(k, CHUNK)
         row[k] = go(remote(p_own.at[:, c], p_side.at[:, c], row_s.at[k], row_r.at[k], behind))
+    for k in range(RAW, steps):
+        c = cols(k, CHUNK)
+        u[k] = go(remote(p_own.at[:, c], u_in.at[:, c], u_s.at[k], u_r.at[k], ahead))
     loads[1].wait()
     for k in range(steps):
         send_tx(k, 0)
-    for k in range(2):
-        send_tx(k, 1)
-    loads[2].wait()
-    h_turned[...] = h_own[...].astype(F32).T.astype(BF16)
-    for load in loads[3:]:
+    for load in loads[2:]:
         load.wait()
-    for k in range(steps):
-        outputs(0, k)
-    for k in range(steps):
-        across_ring(0, k)
-    send_u(0)
-    send_tx(2, 1)
-    for k in range(steps):
-        across_run(0, k)
-    new_params(0)
-    outputs(1, 0)
-    across_ring(1, 0)
-    send_u(1)
-    send_tx(3, 1)
-    new_params(1)
-    outputs(1, 1)
-    across_ring(1, 1)
-    across_run(1, 0)
-    send_u(2)
-    new_params(2)
-    outputs(1, 2)
-    across_ring(1, 2)
-    across_run(1, 1)
-    send_ty(0)
-    send_ty(1)
-    send_u(3)
-    new_params(3)
-    outputs(1, 3)
-    across_ring(1, 3)
-    for k in range(steps):
-        residual(0, k)
-    residual(1, 0)
-    residual(1, 1)
-    across_run(1, 2)
-    send_ty(2)
-    back_ring(0)
-    back_ring(1)
-    across_run(1, 3)
-    send_ty(3)
-    residual(1, 2)
-    residual(1, 3)
-    send_ty(4)
-    send_ty(5)
-    send_ty(6)
-    send_ty(7)
-    back_ring(2)
-    back_core(0)
-    back_core(1)
-    last_grad(0)
-    last_grad(1)
-    back_ring(3)
-    back_core(2)
-    last_grad(2)
-    for k in range(steps):
-        tx[k, 1].wait_recv()
-    for b in range(4):
-        new_tracker(b)
-    back_core(3)
-    last_grad(3)
-    for b in range(4, blocks):
-        new_tracker(b)
+    h_own[...] = h_turned[...].astype(F32).T.astype(BF16)
+    def side_wait():
+        for k in range(steps):
+            tx[k, 1].wait_recv()
+
+    plan = [
+        *[(outputs, 0, k) for k in range(steps)],
+        *[(across_ring, 0, k) for k in range(steps)],
+        (send_u, 0),
+        *[(across_run, 0, k) for k in range(steps)],
+        (send_pair, 2),
+        (new_params, 0),
+        (outputs, 1, 0),
+        (across_ring, 1, 0),
+        (send_pair, 3),
+        (send_u, 1),
+        *[(send_tx, k, 1) for k in range(steps)],
+        (across_run, 1, 0),
+        (new_params, 1),
+        (outputs, 1, 1),
+        (across_ring, 1, 1),
+        (send_ty, 0),
+        (send_ty, 1),
+        (new_params, 2),
+        (outputs, 1, 2),
+        (across_ring, 1, 2),
+        (across_run, 1, 1),
+        (send_ty, 2),
+        (new_params, 3),
+        (outputs, 1, 3),
+        (across_ring, 1, 3),
+        (across_run, 1, 2),
+        (across_run, 1, 3),
+        *[(residual, 0, k) for k in range(steps)],
+        *[(residual, 1, k) for k in range(steps)],
+        *[(back_ring, k) for k in range(steps - 1)],
+        *[(send_ty, b) for b in range(3, blocks)],
+        (back_ring, 3),
+        (side_wait,),
+        (back_core, 0),
+        (back_core, 1),
+        (last_grad, 0),
+        (back_core, 2),
+        (last_grad, 1),
+        (back_core, 3),
+        (last_grad, 2),
+        (last_grad, 3),
+        *[(new_tracker, b) for b in range(blocks)],
+    ]
+    for step, *call in plan:
+        if SCOPES:
+            with jax.named_scope("_".join([step.__name__, *map(str, call)])):
+                step(*call)
+        else:
+            step(*call)
     for copy in sent:
         copy.wait_send()
-    for store in outs:
-        store.wait()
+
+
+def store_kernel(params_near, tracker_near, params_far, tracker_far, sem):
+    copies = [
+        pltpu.make_async_copy(params_near, params_far, sem.at[0]),
+        pltpu.make_async_copy(tracker_near, tracker_far, sem.at[1]),
+    ]
+    for copy in copies:
+        copy.start()
+    for copy in copies:
+        copy.wait()
 
 
 def body(params, tracker, hidden, target):
@@ -315,8 +325,8 @@
     scratch = [
         whole, whole, pltpu.VMEM(hidden.shape, BF16), pltpu.VMEM((steps, strip, PIECE), BF16),
         pltpu.VMEM((rows, tokens), BF16),
-        whole, whole, whole, whole, whole,
-        pltpu.VMEM((2, rows, width), BF16), whole, whole, whole,
+        whole, whole, whole, whole,
+        pltpu.VMEM((2, rows, width), BF16), whole, whole,
         pltpu.VMEM((rows, width), F32),
         pltpu.VMEM((2, steps, CORES, tokens, HALF), BF16), pltpu.VMEM((2, steps, CORES, tokens, HALF), F32),
         pltpu.VMEM((2, steps, tokens, HALF), BF16), pltpu.VMEM((2, steps, tokens, HALF), BF16),
@@ -324,7 +334,7 @@
         pltpu.VMEM((2, steps, strip, HALF), BF16), pltpu.VMEM((2, steps, RUN - 1, strip, PIECE), BF16),
         pltpu.VMEM((steps, strip, PIECE), F32),
         pltpu.VMEM((steps, tokens, HALF), BF16), pltpu.VMEM((steps, tokens, HALF), BF16),
-        dma((3 + steps,)), dma((2, blocks)),
+        dma((3 + steps,)),
     ]
     for shape in (
         (steps,), (steps,), (steps,), (2, steps), (blocks,),
@@ -332,16 +342,26 @@
         (steps, RUN - 1), (steps, RING - 1), (steps,),
     ):
         scratch += [dma(shape), dma(shape)]
-    out = jax.ShapeDtypeStruct((rows, width), BF16)
+    near = pltpu.VMEM((rows, width), BF16)
     params_next, tracker_next = pl.pallas_call(
         step_kernel,
-        out_shape=(out, out),
+        out_shape=(near, near),
         in_specs=[any_] * 4,
-        out_specs=(any_, any_),
+        out_specs=[pl.BlockSpec(memory_space=pltpu.VMEM)] * 2,
         scratch_shapes=scratch,
         name="tracking_step",
-        compiler_params=pltpu.CompilerParams(collective_id=0, has_side_effects=True, vmem_limit_bytes=60 << 20),
-    )(params[0], tracker[0], hidden, target)
+        compiler_params=pltpu.CompilerParams(collective_id=0, has_side_effects=True, vmem_limit_bytes=59 << 20),
+    )(params[0], tracker[0], hidden.T, target)
+    far = jax.ShapeDtypeStruct((rows, width), BF16)
+    params_next, tracker_next = pl.pallas_call(
+        store_kernel,
+        out_shape=(far, far),
+        in_specs=[any_] * 2,
+        out_specs=(any_, any_),
+        scratch_shapes=[dma((2,))],
+        name="store",
+        compiler_params=pltpu.CompilerParams(vmem_limit_bytes=1 << 20),
+    )(params_next, tracker_next)
     return params_next[None], tracker_next[None]
 
 

time: 125 us -> 107 us (0.86)
  the two profiles are of different devices: /device:TPU:1 before, /device:TPU:14 now
where the time goes in v2:
time: 107 us
  Pallas kernels  106 us (99%)
    pallas_call x1, Pallas kernels, body(): pl.pallas_call(step_kernel, out_shape=(near, near), in_specs=[any_] * 4,...  105 us

profile of v2, /device:TPU:14, one launch (start us, length us, event | category | flops | bytes accessed | tf_op | source)
XLA Modules:
  0.0 107.0 jit_solution(201040359942654858)
XLA Ops:
  0.6 105.1 %tracking_step.1 = (bf16[112,4096]{1,0:T(8,128)(2,1)S(1)}, bf16[112,4096]{1,0:T(8,128)(2,1)S(1)}) custom-call(bf16[112,4096]{1,0:T(8,128)(2,1)} %bitcast.5, bf16[112,4096]{1,0:T(8,128)(2,1)} %bitcast.6, bf16[112,128]{1,0:T(8,128)(2,1)} %bitcast.7, bf16[128,4096]{1,0:T(8,128)(2,1)} %target.1), custom_call_target="tpu_custom_call" | custom-call | tf_op jit(solution)/shard_map/tracking_step/pallas_call | solution.py:346
  105.7 1.2 %store.1 = (bf16[112,4096]{1,0:T(8,128)(2,1)}, bf16[112,4096]{1,0:T(8,128)(2,1)}) custom-call(bf16[112,4096]{1,0:T(8,128)(2,1)S(1)} %get-tuple-element.6.params_near, bf16[112,4096]{1,0:T(8,128)(2,1)S(1)} %get-tuple-element.7.tracker_near), custom_call_target="tpu_custom_call" | custom-call | tf_op jit(solution)/shard_map/store/pallas_call | solution.py:356

commit v3 on v2

--- a/solution.py
+++ b/solution.py
@@ -14,6 +14,7 @@
 RING = 8
 CORES = 2
 SCOPES = False
+BLOCK = 256
 RAW = 2
 CHUNK = 1024
 HALF = CHUNK // CORES
@@ -30,14 +31,14 @@
     core_out, core_keep, core_in, z_out, z_in, y_out, y_in, resid_old,
     gather_own, gather_other,
     in_sem,
-    pair_s, pair_r, row_s, row_r, u_s, u_r, tx_s, tx_r, ty_s, ty_r,
-    core_s, core_r, z_s, z_r, y_s, y_r, gy_s, gy_r, gz_s, gz_r, gc_s, gc_r,
+    pair_r, row_r, u_r, tx_r, ty_r, core_r, z_r, y_r, gy_r, gz_r, gc_r,
+    pair_s, row_s, u_s, tx_s, ty_s, core_s, z_s, y_s, gy_s, gz_s, gc_s,
 ):
     rows, width = p_own.shape
     tokens = h_own.shape[0]
     strip = tokens // RING
     steps = width // CHUNK
-    blocks = width // HALF
+    blocks = width // BLOCK
     group, place = lax.axis_index("grp"), lax.axis_index("blk")
     n_grp = lax.axis_size("grp")
     columns = n_grp // 2
@@ -73,7 +74,7 @@
         pltpu.make_async_copy(hidden, h_turned, in_sem.at[2]),
     ] + [
         pltpu.make_async_copy(
-            target.at[ring_rows, pl.ds(piece_column(k), PIECE)], tgt.at[k], in_sem.at[3 + k]
+            target.at[ring_rows, pl.ds(piece_column(k), PIECE)], tgt.at[k], in_sem.at[3]
         )
         for k in range(steps)
     ]
@@ -101,20 +102,20 @@
     c_behind = valid(group - 2 * s) / 9.0
     c_next = (keep(group + s) + keep(group + 2 * s)) * third * valid(group + 2 * s)
 
-    sent = []
-
     def go(copy):
         copy.start()
-        sent.append(copy)
         return copy
 
+    def all_of(ref, sem):
+        pltpu.make_async_copy(ref, ref, sem).wait()
+
     pair, row, u, tx, ty = {}, {}, {}, {}, {}
-    core_copy, z_copy, y_copy, gy, gz, gc = {}, {}, {}, {}, {}, {}
+    core_copy, gc = {}, {}
 
     def send_tx(k, d):
         c = cols(k, CHUNK)
         tx[k, d] = go(remote(
-            t_own.at[:, c], t_side.at[d, :, c], tx_s.at[d, k], tx_r.at[d, k], behind if d == 0 else ahead
+            t_own.at[:, c], t_side.at[d, :, c], tx_s, tx_r.at[k if d == 0 else steps], behind if d == 0 else ahead
         ))
 
     def outputs(p, k):
@@ -125,7 +126,7 @@
             core_keep[p, k, half] = part
             core_out[p, k, half] = part.astype(BF16)
         core_copy[p, k] = go(remote(
-            core_out.at[p, k, 1 - core], core_in.at[p, k], core_s.at[p, k], core_r.at[p, k], partner
+            core_out.at[p, k, 1 - core], core_in.at[p, k], core_s, core_r.at[p, k], partner
         ))
 
     def across_ring(p, k):
@@ -133,28 +134,27 @@
         z_out[p, k] = (core_keep[p, k, core] + core_in[p, k].astype(F32)).astype(BF16)
         for j in range(RING - 1):
             part = pl.ds(pl.multiple_of(ring_at[j] * strip, strip), strip)
-            z_copy[p, k, j] = go(remote(
-                z_out.at[p, k, part], z_in.at[p, k, j], z_s.at[p, k, j], z_r.at[p, k, j], ring_peer[j]
-            ))
+            remote(z_out.at[p, k, part], z_in.at[p, k, j], z_s, z_r.at[p, k], ring_peer[j]).start()
 
     def across_run(p, k):
         total = z_out[p, k, ring_rows].astype(F32)
+        all_of(z_in.at[p, k], z_r.at[p, k])
         for j in range(RING - 1):
-            z_copy[p, k, j].wait_recv()
             total += z_in[p, k, j].astype(F32)
         y_out[p, k] = total.astype(BF16)
         for j in range(RUN - 1):
             part = pl.ds(pl.multiple_of(run_at[j] * PIECE, PIECE), PIECE)
-            y_copy[p, k, j] = go(remote(
-                y_out.at[p, k, :, part], y_in.at[p, k, j], y_s.at[p, k, j], y_r.at[p, k, j], run_peer[j]
-            ))
+            remote(y_out.at[p, k, :, part], y_in.at[p, k, j], y_s, y_r.at[k if p else steps], run_peer[j]).start()
 
     own_piece = pl.ds(pl.multiple_of(run * PIECE, PIECE), PIECE)
 
     def residual(p, k):
         total = y_out[p, k, :, own_piece].astype(F32)
+        if p:
+            all_of(y_in.at[p, k], y_r.at[k])
+        elif k == 0:
+            all_of(y_in.at[p], y_r.at[steps])
         for j in range(RUN - 1):
-            y_copy[p, k, j].wait_recv()
             total += y_in[p, k, j].astype(F32)
         resid = jnp.tanh(total - tgt[k].astype(F32))
         if p == 0:
@@ -163,19 +163,17 @@
         gather_own[k, ring_rows, own_piece] = (resid - resid_old[k]).astype(BF16)
         block = gather_own.at[k, ring_rows, own_piece]
         for j in range(RUN - 1):
-            gy[k, j] = go(remote(block, block, gy_s.at[k, j], gy_r.at[k, j], run_peer[j]))
+            remote(block, block, gy_s, gy_r.at[k], run_peer[j]).start()
 
     def back_ring(k):
-        for j in range(RUN - 1):
-            gy[k, j].wait_recv()
+        all_of(y_in.at[1, k], gy_r.at[k])
         block = gather_own.at[k, ring_rows]
         for j in range(RING - 1):
-            gz[k, j] = go(remote(block, block, gz_s.at[k, j], gz_r.at[k, j], ring_peer[j]))
+            remote(block, block, gz_s, gz_r.at[k], ring_peer[j]).start()
 
     def back_core(k):
-        for j in range(RING - 1):
-            gz[k, j].wait_recv()
-        gc[k] = go(remote(gather_own.at[k], gather_other.at[k], gc_s.at[k], gc_r.at[k], partner))
+        all_of(z_in.at[1, k], gz_r.at[k])
+        gc[k] = go(remote(gather_own.at[k], gather_other.at[k], gc_s, gc_r.at[k], partner))
         c = pl.ds(pl.multiple_of(k * CHUNK + core * HALF, HALF), HALF)
         grad[:, c] = jnp.dot(h_turned[...], gather_own[k], preferred_element_type=F32)
 
@@ -188,7 +186,7 @@
         c = cols(k, CHUNK)
         pair[k].wait_recv()
         u_out[:, c] = (c_ahead * p_own[:, c].astype(F32) + c_next * p_across[:, c].astype(F32)).astype(BF16)
-        u[k] = go(remote(u_out.at[:, c], u_in.at[:, c], u_s.at[k], u_r.at[k], ahead))
+        u[k] = go(remote(u_out.at[:, c], u_in.at[:, c], u_s, u_r.at[k], ahead))
 
     def send_pair(k):
         c = cols(k, CHUNK)
@@ -197,7 +195,7 @@
             row[k].wait_recv()
             block = u_out
             u_out[:, c] = (c_pair * p_own[:, c].astype(F32) + c_next * p_side[:, c].astype(F32)).astype(BF16)
-        pair[k] = go(remote(block.at[:, c], p_across.at[:, c], pair_s.at[k], pair_r.at[k], across))
+        pair[k] = go(remote(block.at[:, c], p_across.at[:, c], pair_s, pair_r.at[k], across))
 
     def new_params(k):
         c = cols(k, CHUNK)
@@ -213,21 +211,29 @@
 
     seen = set()
 
-    def send_ty(b):
-        k = b * HALF // CHUNK
-        if k not in seen:
-            tx[k, 0].wait_recv()
-            seen.add(k)
-        c = cols(b, HALF)
-        w_out[:, c] = (c_pair * t_own[:, c].astype(F32) + c_next * t_side[0, :, c].astype(F32)).astype(BF16)
-        ty[b] = go(remote(w_out.at[:, c], w_in.at[:, c], ty_s.at[b], ty_r.at[b], across))
+    def send_ty(first, last):
+        for b in range(first, last):
+            k = b * BLOCK // CHUNK
+            if k not in seen:
+                tx[k, 0].wait_recv()
+                seen.add(k)
+            c = cols(b, BLOCK)
+            w_out[:, c] = (c_pair * t_own[:, c].astype(F32) + c_next * t_side[0, :, c].astype(F32)).astype(BF16)
+            ty[b] = go(remote(w_out.at[:, c], w_in.at[:, c], ty_s, ty_r.at[b], across))
 
     def new_tracker(b):
-        c = cols(b, HALF)
+        c = cols(b, BLOCK)
         ty[b].wait_recv()
         mixed = c_own * t_own[:, c].astype(F32) + c_ahead * t_side[0, :, c].astype(F32)
         mixed += c_behind * t_side[1, :, c].astype(F32) + w_in[:, c].astype(F32)
         tracker_next[:, c] = (mixed + grad[:, c] * (1.0 / tokens)).astype(BF16)
+
+    def drain():
+        for ref, sem in (
+            (p_own, pair_s), (p_own, row_s), (p_own, u_s), (t_side, tx_s),
+            (core_in, core_s), (z_in, z_s), (y_in, y_s), (y_in.at[1], gy_s), (z_in.at[1], gz_s), (gather_own, gc_s),
+        ):
+            all_of(ref, sem)
 
     loads[0].wait()
     pl.semaphore_wait(barrier, len(peers))
@@ -235,19 +241,18 @@
         send_pair(k)
     for k in range(steps):
         c = cols(k, CHUNK)
-        row[k] = go(remote(p_own.at[:, c], p_side.at[:, c], row_s.at[k], row_r.at[k], behind))
+        row[k] = go(remote(p_own.at[:, c], p_side.at[:, c], row_s, row_r.at[k], behind))
     for k in range(RAW, steps):
         c = cols(k, CHUNK)
-        u[k] = go(remote(p_own.at[:, c], u_in.at[:, c], u_s.at[k], u_r.at[k], ahead))
+        u[k] = go(remote(p_own.at[:, c], u_in.at[:, c], u_s, u_r.at[k], ahead))
     loads[1].wait()
     for k in range(steps):
         send_tx(k, 0)
-    for load in loads[2:]:
-        load.wait()
+    loads[2].wait()
+    all_of(tgt, in_sem.at[3])
     h_own[...] = h_turned[...].astype(F32).T.astype(BF16)
     def side_wait():
-        for k in range(steps):
-            tx[k, 1].wait_recv()
+        all_of(t_side.at[1], tx_r.at[steps])
 
     plan = [
         *[(outputs, 0, k) for k in range(steps)],
@@ -265,22 +270,22 @@
         (new_params, 1),
         (outputs, 1, 1),
         (across_ring, 1, 1),
-        (send_ty, 0),
-        (send_ty, 1),
+        (send_ty, 0, 4),
         (new_params, 2),
         (outputs, 1, 2),
         (across_ring, 1, 2),
         (across_run, 1, 1),
-        (send_ty, 2),
+        (send_ty, 4, 6),
         (new_params, 3),
         (outputs, 1, 3),
         (across_ring, 1, 3),
         (across_run, 1, 2),
         (across_run, 1, 3),
+        (send_ty, 6, 7),
         *[(residual, 0, k) for k in range(steps)],
         *[(residual, 1, k) for k in range(steps)],
         *[(back_ring, k) for k in range(steps - 1)],
-        *[(send_ty, b) for b in range(3, blocks)],
+        (send_ty, 7, blocks),
         (back_ring, 3),
         (side_wait,),
         (back_core, 0),
@@ -291,6 +296,7 @@
         (back_core, 3),
         (last_grad, 2),
         (last_grad, 3),
+        (drain,),
         *[(new_tracker, b) for b in range(blocks)],
     ]
     for step, *call in plan:
@@ -299,8 +305,7 @@
                 step(*call)
         else:
             step(*call)
-    for copy in sent:
-        copy.wait_send()
+    all_of(w_out, ty_s)
 
 
 def store_kernel(params_near, tracker_near, params_far, tracker_far, sem):
@@ -317,7 +322,7 @@
 def body(params, tracker, hidden, target):
     _, rows, width = params.shape
     tokens = hidden.shape[0]
-    steps, blocks = width // CHUNK, width // HALF
+    steps, blocks = width // CHUNK, width // BLOCK
     strip = tokens // RING
     any_ = pl.BlockSpec(memory_space=pl.ANY)
     dma = pltpu.SemaphoreType.DMA
@@ -334,14 +339,11 @@
         pltpu.VMEM((2, steps, strip, HALF), BF16), pltpu.VMEM((2, steps, RUN - 1, strip, PIECE), BF16),
         pltpu.VMEM((steps, strip, PIECE), F32),
         pltpu.VMEM((steps, tokens, HALF), BF16), pltpu.VMEM((steps, tokens, HALF), BF16),
-        dma((3 + steps,)),
+        dma((4,)),
     ]
-    for shape in (
-        (steps,), (steps,), (steps,), (2, steps), (blocks,),
-        (2, steps), (2, steps, RING - 1), (2, steps, RUN - 1),
-        (steps, RUN - 1), (steps, RING - 1), (steps,),
-    ):
-        scratch += [dma(shape), dma(shape)]
+    scratch += [dma((steps,)), dma((steps,)), dma((steps,)), dma((steps + 1,)), dma((blocks,))]
+    scratch += [dma((2, steps)), dma((2, steps)), dma((steps + 1,)), dma((steps,)), dma((steps,)), dma((steps,))]
+    scratch += [dma(())] * 11
     near = pltpu.VMEM((rows, width), BF16)
     params_next, tracker_next = pl.pallas_call(
         step_kernel,

time: 107 us -> 104 us (0.972)
  the two profiles are of different devices: /device:TPU:14 before, /device:TPU:59 now
where the time goes in v3:
time: 104 us
  Pallas kernels  103 us (99%)
    pallas_call x1, Pallas kernels, body(): pl.pallas_call(step_kernel, out_shape=(near, near), in_specs=[any_] * 4,...  102 us

profile of v3, /device:TPU:59, one launch (start us, length us, event | category | flops | bytes accessed | tf_op | source)
XLA Modules:
  0.0 103.7 jit_solution(4475491090690578409)
XLA Ops:
  0.6 101.8 %tracking_step.1 = (bf16[112,4096]{1,0:T(8,128)(2,1)S(1)}, bf16[112,4096]{1,0:T(8,128)(2,1)S(1)}) custom-call(bf16[112,4096]{1,0:T(8,128)(2,1)} %bitcast.5, bf16[112,4096]{1,0:T(8,128)(2,1)} %bitcast.6, bf16[112,128]{1,0:T(8,128)(2,1)} %bitcast.7, bf16[128,4096]{1,0:T(8,128)(2,1)} %target.1), custom_call_target="tpu_custom_call" | custom-call | tf_op jit(solution)/shard_map/tracking_step/pallas_call | solution.py:348
  102.5 1.2 %store.1 = (bf16[112,4096]{1,0:T(8,128)(2,1)}, bf16[112,4096]{1,0:T(8,128)(2,1)}) custom-call(bf16[112,4096]{1,0:T(8,128)(2,1)S(1)} %get-tuple-element.6.params_near, bf16[112,4096]{1,0:T(8,128)(2,1)S(1)} %get-tuple-element.7.tracker_near), custom_call_target="tpu_custom_call" | custom-call | tf_op jit(solution)/shard_map/store/pallas_call | solution.py:358

commit v4 on v3

--- a/solution.py
+++ b/solution.py
@@ -33,6 +33,7 @@
     in_sem,
     pair_r, row_r, u_r, tx_r, ty_r, core_r, z_r, y_r, gy_r, gz_r, gc_r,
     pair_s, row_s, u_s, tx_s, ty_s, core_s, z_s, y_s, gy_s, gz_s, gc_s,
+    met,
 ):
     rows, width = p_own.shape
     tokens = h_own.shape[0]
@@ -60,9 +61,15 @@
     behind = (lax.rem(x - s + columns, columns) * 2 + side, place)
 
     barrier = pltpu.get_barrier_semaphore()
-    peers = [across, ahead, behind, partner] + run_peer + ring_peer
+    peers = [across, ahead, behind, partner] + run_peer
     for peer in peers:
         pl.semaphore_signal(barrier, inc=1, device_id=peer, device_id_type=MESH)
+
+    def greet(sem, j):
+        pl.semaphore_signal(sem, inc=1, device_id=ring_peer[j], device_id_type=MESH)
+
+    for j in range(RING - 1):
+        pl.when(ring_at[j] > ring)(lambda: greet(barrier, j))
 
     def piece_column(k):
         return pl.multiple_of(k * CHUNK + core * HALF + run * PIECE, PIECE)
@@ -128,6 +135,11 @@
         core_copy[p, k] = go(remote(
             core_out.at[p, k, 1 - core], core_in.at[p, k], core_s, core_r.at[p, k], partner
         ))
+
+    def ring_met():
+        @pl.when(ring < RING - 1)
+        def _():
+            pl.semaphore_wait(met, RING - 1 - ring)
 
     def across_ring(p, k):
         core_copy[p, k].wait_recv()
@@ -236,7 +248,9 @@
             all_of(ref, sem)
 
     loads[0].wait()
-    pl.semaphore_wait(barrier, len(peers))
+    pl.semaphore_wait(barrier, len(peers) + ring)
+    for j in range(RING - 1):
+        pl.when(ring_at[j] < ring)(lambda: greet(met, j))
     for k in range(RAW):
         send_pair(k)
     for k in range(steps):
@@ -256,36 +270,39 @@
 
     plan = [
         *[(outputs, 0, k) for k in range(steps)],
+        (ring_met,),
         *[(across_ring, 0, k) for k in range(steps)],
         (send_u, 0),
-        *[(across_run, 0, k) for k in range(steps)],
         (send_pair, 2),
         (new_params, 0),
         (outputs, 1, 0),
+        (send_pair, 3),
+        *[(across_run, 0, k) for k in range(steps)],
         (across_ring, 1, 0),
-        (send_pair, 3),
         (send_u, 1),
         *[(send_tx, k, 1) for k in range(steps)],
         (across_run, 1, 0),
         (new_params, 1),
         (outputs, 1, 1),
+        (send_ty, 0, 4),
         (across_ring, 1, 1),
-        (send_ty, 0, 4),
         (new_params, 2),
         (outputs, 1, 2),
         (across_ring, 1, 2),
+        (send_ty, 4, 7),
         (across_run, 1, 1),
-        (send_ty, 4, 6),
         (new_params, 3),
         (outputs, 1, 3),
         (across_ring, 1, 3),
         (across_run, 1, 2),
         (across_run, 1, 3),
-        (send_ty, 6, 7),
+        (send_ty, 7, 8),
         *[(residual, 0, k) for k in range(steps)],
         *[(residual, 1, k) for k in range(steps)],
-        *[(back_ring, k) for k in range(steps - 1)],
-        (send_ty, 7, blocks),
+        (back_ring, 0),
+        (back_ring, 1),
+        (back_ring, 2),
+        (send_ty, 8, blocks),
         (back_ring, 3),
         (side_wait,),
         (back_core, 0),
@@ -343,7 +360,7 @@
     ]
     scratch += [dma((steps,)), dma((steps,)), dma((steps,)), dma((steps + 1,)), dma((blocks,))]
     scratch += [dma((2, steps)), dma((2, steps)), dma((steps + 1,)), dma((steps,)), dma((steps,)), dma((steps,))]
-    scratch += [dma(())] * 11
+    scratch += [dma(())] * 11 + [pltpu.SemaphoreType.REGULAR]
     near = pltpu.VMEM((rows, width), BF16)
     params_next, tracker_next = pl.pallas_call(
         step_kernel,

time: 104 us -> 101 us (0.971)
  the two profiles are of different devices: /device:TPU:59 before, /device:TPU:1 now
where the time goes in v4:
time: 101 us
  Pallas kernels  100 us (99%)
    pallas_call x1, Pallas kernels, body(): pl.pallas_call(step_kernel, out_shape=(near, near), in_specs=[any_] * 4,...  99.2 us

profile of v4, /device:TPU:1, one launch (start us, length us, event | category | flops | bytes accessed | tf_op | source)
XLA Modules:
  0.0 101.1 jit_solution(2776071877913005305)
XLA Ops:
  0.6 99.2 %tracking_step.1 = (bf16[112,4096]{1,0:T(8,128)(2,1)S(1)}, bf16[112,4096]{1,0:T(8,128)(2,1)S(1)}) custom-call(bf16[112,4096]{1,0:T(8,128)(2,1)} %bitcast.5, bf16[112,4096]{1,0:T(8,128)(2,1)} %bitcast.6, bf16[112,128]{1,0:T(8,128)(2,1)} %bitcast.7, bf16[128,4096]{1,0:T(8,128)(2,1)} %target.1), custom_call_target="tpu_custom_call" | custom-call | tf_op jit(solution)/shard_map/tracking_step/pallas_call | solution.py:365
  99.8 1.2 %store.1 = (bf16[112,4096]{1,0:T(8,128)(2,1)}, bf16[112,4096]{1,0:T(8,128)(2,1)}) custom-call(bf16[112,4096]{1,0:T(8,128)(2,1)S(1)} %get-tuple-element.6.params_near, bf16[112,4096]{1,0:T(8,128)(2,1)S(1)} %get-tuple-element.7.tracker_near), custom_call_target="tpu_custom_call" | custom-call | tf_op jit(solution)/shard_map/store/pallas_call | solution.py:375

commit v5 on v4

--- a/solution.py
+++ b/solution.py
@@ -231,11 +231,12 @@
                 seen.add(k)
             c = cols(b, BLOCK)
             w_out[:, c] = (c_pair * t_own[:, c].astype(F32) + c_next * t_side[0, :, c].astype(F32)).astype(BF16)
-            ty[b] = go(remote(w_out.at[:, c], w_in.at[:, c], ty_s, ty_r.at[b], across))
+            ty[b] = go(remote(w_out.at[:, c], w_in.at[:, c], ty_s, ty_r.at[b // 2], across))
 
     def new_tracker(b):
         c = cols(b, BLOCK)
-        ty[b].wait_recv()
+        if b % 2 == 0:
+            all_of(w_in.at[:, cols(b // 2, 2 * BLOCK)], ty_r.at[b // 2])
         mixed = c_own * t_own[:, c].astype(F32) + c_ahead * t_side[0, :, c].astype(F32)
         mixed += c_behind * t_side[1, :, c].astype(F32) + w_in[:, c].astype(F32)
         tracker_next[:, c] = (mixed + grad[:, c] * (1.0 / tokens)).astype(BF16)
@@ -301,8 +302,8 @@
         *[(residual, 1, k) for k in range(steps)],
         (back_ring, 0),
         (back_ring, 1),
+        (send_ty, 8, blocks),
         (back_ring, 2),
-        (send_ty, 8, blocks),
         (back_ring, 3),
         (side_wait,),
         (back_core, 0),
@@ -358,7 +359,7 @@
         pltpu.VMEM((steps, tokens, HALF), BF16), pltpu.VMEM((steps, tokens, HALF), BF16),
         dma((4,)),
     ]
-    scratch += [dma((steps,)), dma((steps,)), dma((steps,)), dma((steps + 1,)), dma((blocks,))]
+    scratch += [dma((steps,)), dma((steps,)), dma((steps,)), dma((steps + 1,)), dma((blocks // 2,))]
     scratch += [dma((2, steps)), dma((2, steps)), dma((steps + 1,)), dma((steps,)), dma((steps,)), dma((steps,))]
     scratch += [dma(())] * 11 + [pltpu.SemaphoreType.REGULAR]
     near = pltpu.VMEM((rows, width), BF16)

time: 101 us -> 101 us (level)
  no operation moved by 1% of the time
where the time goes in v5:
time: 101 us
  Pallas kernels  100 us (99%)
    pallas_call x1, Pallas kernels, body(): pl.pallas_call(step_kernel, out_shape=(near, near), in_specs=[any_] * 4,...  98.8 us

profile of v5, /device:TPU:1, one launch (start us, length us, event | category | flops | bytes accessed | tf_op | source)
XLA Modules:
  0.0 100.7 jit_solution(11847100400333680624)
XLA Ops:
  0.6 98.8 %tracking_step.1 = (bf16[112,4096]{1,0:T(8,128)(2,1)S(1)}, bf16[112,4096]{1,0:T(8,128)(2,1)S(1)}) custom-call(bf16[112,4096]{1,0:T(8,128)(2,1)} %bitcast.5, bf16[112,4096]{1,0:T(8,128)(2,1)} %bitcast.6, bf16[112,128]{1,0:T(8,128)(2,1)} %bitcast.7, bf16[128,4096]{1,0:T(8,128)(2,1)} %target.1), custom_call_target="tpu_custom_call" | custom-call | tf_op jit(solution)/shard_map/tracking_step/pallas_call | solution.py:366
  99.4 1.2 %store.1 = (bf16[112,4096]{1,0:T(8,128)(2,1)}, bf16[112,4096]{1,0:T(8,128)(2,1)}) custom-call(bf16[112,4096]{1,0:T(8,128)(2,1)S(1)} %get-tuple-element.6.params_near, bf16[112,4096]{1,0:T(8,128)(2,1)S(1)} %get-tuple-element.7.tracker_near), custom_call_target="tpu_custom_call" | custom-call | tf_op jit(solution)/shard_map/store/pallas_call | solution.py:376
